TPU v7x, 32 devices: a whole 2x2x4 slice. The times are simulated.
32 devices in a mesh: group: 8 (over z, x), local: 4 (over y, core).
Axes of the slice: x: 2, y: 2, z: 4, core: 2. Of those that a mesh axis runs over, the one named last changes fastest.
Arguments:
- ids: int32 [4096, 32, 8], P(('group', 'local')), may hold values from 0 to 4095
- lengths: int32 [4096, 32], P(('group', 'local')), may hold values from 1 to 8, as said below
- id_weights: float32 [4096, 32, 8], P(('group', 'local')), may hold values from 0.5 to 1.5
- table: float32 [131072, 256], P(('group', 'local')), may hold values from -2.4 to 2.4
Outputs:
- pooled: float32 [4096, 32, 256], P(('group', 'local'))
Inputs may be any that keep to these rules, and one draw needn't show every extreme that they name: `lengths`: every draw has some bag with 8 live ids.
All inputs are finite; a program needn't handle non-finite values.
Results may differ from a plain program's by a relative error of at most 0.00002.
Values sent between devices are 32-bit elements; how exact they have to be, the bound alone decides.
No kernel may reach another device: no remote copies, remote signals or barrier semaphores. Data moves between devices by JAX's collectives and lax.ppermute only.
A program may use at most 128 MiB of HBM per device.

v0:
```python
import jax
import jax.numpy as jnp
from jax import lax
from jax.sharding import PartitionSpec as P


def pool_block(table, pair):
    rows = jnp.take(table, pair[0], axis=0)
    return jnp.sum(rows * pair[1][:, :, None], axis=1)


def partial_pool(table):

    def apply_block(pair):
        return pool_block(table, pair)

    return apply_block


def body(ids, lengths, id_weights, table):
    examples, tables, bag = ids.shape
    n_group = lax.axis_size("group")
    n_local = lax.axis_size("local")
    devices = n_group * n_local
    tab_dev = tables // devices
    rows_each = table.shape[0] // tab_dev
    width = table.shape[1]
    slot = lax.broadcasted_iota(jnp.int32, ids.shape, 2)
    masked = jnp.where(slot < lengths[:, :, None], id_weights, jnp.zeros_like(id_weights))
    packed = jnp.concatenate([ids.astype(jnp.float32), masked], axis=2)
    arrived = lax.all_to_all(packed, ("group", "local"), split_axis=1, concat_axis=0, tiled=True)
    offsets = (jnp.arange(tab_dev, dtype=jnp.int32) * rows_each)[None, :, None]
    index = arrived[:, :, :bag].astype(jnp.int32) + offsets
    weights = arrived[:, :, bag:]
    per_step = max(1, 512 // (examples * tab_dev))
    while devices % per_step:
        per_step = per_step // 2
    blocks = devices // per_step
    block_rows = per_step * examples * tab_dev
    pooled = lax.map(
        partial_pool(table),
        (index.reshape(blocks, block_rows, bag), weights.reshape(blocks, block_rows, bag)),
    )
    pooled = pooled.reshape(devices * examples, tab_dev, width)
    result = lax.all_to_all(pooled, ("group", "local"), split_axis=0, concat_axis=1, tiled=True)
    return result


def solution(mesh):
    placed = (
        P(("group", "local"), None, None),
        P(("group", "local"), None),
        P(("group", "local"), None, None),
        P(("group", "local"), None),
    )
    return jax.shard_map(
        body,
        mesh=mesh,
        in_specs=placed,
        out_specs=P(("group", "local"), None, None),
        check_vma=False,
    )
```

profile of v0, /device:TPU:0, one launch (start us, length us, event | category | flops | bytes accessed | tf_op | source)
XLA Modules:
  0.0 332.3 jit_solution(10436769486742888752)
XLA Ops:
  2.6 7.3 %all-to-all-start = ((f32[128,32,16]{0,2,1:T(8,128)}), f32[128,32,16]{0,2,1:T(8,128)S(1)}, u32[]{:S(2)}, u32[]{:S(2)}) async-start(f32[128,32,16]{0,2,1:T(8,128)} %pad_maximum_fusion), calls=%async_computation | async-start | bytes 524288 | tf_op jit(solution)/shard_map/all_to_all | solution.py:31
  9.9 10.6 %all-to-all-done = f32[128,32,16]{0,2,1:T(8,128)S(1)} async-done(((f32[128,32,16]{0,2,1:T(8,128)}), f32[128,32,16]{0,2,1:T(8,128)S(1)}, u32[]{:S(2)}, u32[]{:S(2)}) %all-to-all-start) | async-done | bytes 262176 | tf_op jit(solution)/shard_map/all_to_all | solution.py:31
  20.7 1.9 copy.15
  23.2 200.9 %while.10 = (s32[]{:T(128)}, f32[8,512,256]{2,1,0:T(8,128)}, s32[8,512,8]{2,1,0:T(8,128)S(1)}, f32[4096,256]{1,0:T(8,128)}, f32[8,512,8]{2,1,0:T(8,128)}, /*index=5*/s32[]{:T(128)}) while((s32[]{:T(128)}, f32[8,512,256]{2,1,0:T(8,128)}, s32[8,512,8]{2,1,0:T(8,128)S(1)}, f32[4096,256]{1,0:T(8,128)}, f32[8,512,8]{2,1,0:T(8,128)}, ...), condition=%wide.region_2.3_spmd, body=%wide.region_0.2_spmd.sunk | while | flops 3055618 | bytes 14344785 | solution.py:40
  23.4 18.3 %gather_fusion = f32[4096,256]{1,0:T(8,128)} fusion(f32[4096,256]{1,0:T(8,128)} %get-tuple-element.101, s32[4096]{0:T(1024)S(1)} %broadcast_clamp_fusion.2), kind=kCustom, calls=%fused_computation.clone.1 | custom fusion | bytes 8404992 | tf_op jit(solution)/shard_map/while/body/eval_jaxpr/jit(_take)/gather | solution.py:8
  42.8 4.7 %fusion.5 = f32[512,256]{1,0:T(8,128)S(1)} fusion(f32[4096,256]{1,0:T(8,128)} %gather_fusion, f32[512,8]{1,0:T(8,128)S(1)} %dynamic-slice_bitcast_fusion.2, pred[512,8]{1,0:T(8,128)(4,1)S(1)} %compare_and_fusion.2), kind=kLoop, calls=%fused_computation.3.clone.1 | loop fusion | flops 3014656 | bytes 4739072 | tf_op jit(solution)/shard_map/while/body/eval_jaxpr/reduce_sum | solution.py:9
  48.5 18.3 %gather_fusion = f32[4096,256]{1,0:T(8,128)} fusion(f32[4096,256]{1,0:T(8,128)} %get-tuple-element.101, s32[4096]{0:T(1024)S(1)} %broadcast_clamp_fusion.2), kind=kCustom, calls=%fused_computation.clone.1 | custom fusion | bytes 8404992 | tf_op jit(solution)/shard_map/while/body/eval_jaxpr/jit(_take)/gather | solution.py:8
  67.9 4.7 %fusion.5 = f32[512,256]{1,0:T(8,128)S(1)} fusion(f32[4096,256]{1,0:T(8,128)} %gather_fusion, f32[512,8]{1,0:T(8,128)S(1)} %dynamic-slice_bitcast_fusion.2, pred[512,8]{1,0:T(8,128)(4,1)S(1)} %compare_and_fusion.2), kind=kLoop, calls=%fused_computation.3.clone.1 | loop fusion | flops 3014656 | bytes 4739072 | tf_op jit(solution)/shard_map/while/body/eval_jaxpr/reduce_sum | solution.py:9
  73.6 18.3 %gather_fusion = f32[4096,256]{1,0:T(8,128)} fusion(f32[4096,256]{1,0:T(8,128)} %get-tuple-element.101, s32[4096]{0:T(1024)S(1)} %broadcast_clamp_fusion.2), kind=kCustom, calls=%fused_computation.clone.1 | custom fusion | bytes 8404992 | tf_op jit(solution)/shard_map/while/body/eval_jaxpr/jit(_take)/gather | solution.py:8
  92.0 1.0 dynamic-slice_bitcast_fusion.2
  93.0 4.7 %fusion.5 = f32[512,256]{1,0:T(8,128)S(1)} fusion(f32[4096,256]{1,0:T(8,128)} %gather_fusion, f32[512,8]{1,0:T(8,128)S(1)} %dynamic-slice_bitcast_fusion.2, pred[512,8]{1,0:T(8,128)(4,1)S(1)} %compare_and_fusion.2), kind=kLoop, calls=%fused_computation.3.clone.1 | loop fusion | flops 3014656 | bytes 4739072 | tf_op jit(solution)/shard_map/while/body/eval_jaxpr/reduce_sum | solution.py:9
  98.8 18.3 %gather_fusion = f32[4096,256]{1,0:T(8,128)} fusion(f32[4096,256]{1,0:T(8,128)} %get-tuple-element.101, s32[4096]{0:T(1024)S(1)} %broadcast_clamp_fusion.2), kind=kCustom, calls=%fused_computation.clone.1 | custom fusion | bytes 8404992 | tf_op jit(solution)/shard_map/while/body/eval_jaxpr/jit(_take)/gather | solution.py:8
  118.1 4.7 %fusion.5 = f32[512,256]{1,0:T(8,128)S(1)} fusion(f32[4096,256]{1,0:T(8,128)} %gather_fusion, f32[512,8]{1,0:T(8,128)S(1)} %dynamic-slice_bitcast_fusion.2, pred[512,8]{1,0:T(8,128)(4,1)S(1)} %compare_and_fusion.2), kind=kLoop, calls=%fused_computation.3.clone.1 | loop fusion | flops 3014656 | bytes 4739072 | tf_op jit(solution)/shard_map/while/body/eval_jaxpr/reduce_sum | solution.py:9
  123.9 18.3 %gather_fusion = f32[4096,256]{1,0:T(8,128)} fusion(f32[4096,256]{1,0:T(8,128)} %get-tuple-element.101, s32[4096]{0:T(1024)S(1)} %broadcast_clamp_fusion.2), kind=kCustom, calls=%fused_computation.clone.1 | custom fusion | bytes 8404992 | tf_op jit(solution)/shard_map/while/body/eval_jaxpr/jit(_take)/gather | solution.py:8
  143.2 4.7 %fusion.5 = f32[512,256]{1,0:T(8,128)S(1)} fusion(f32[4096,256]{1,0:T(8,128)} %gather_fusion, f32[512,8]{1,0:T(8,128)S(1)} %dynamic-slice_bitcast_fusion.2, pred[512,8]{1,0:T(8,128)(4,1)S(1)} %compare_and_fusion.2), kind=kLoop, calls=%fused_computation.3.clone.1 | loop fusion | flops 3014656 | bytes 4739072 | tf_op jit(solution)/shard_map/while/body/eval_jaxpr/reduce_sum | solution.py:9
  149.0 18.3 %gather_fusion = f32[4096,256]{1,0:T(8,128)} fusion(f32[4096,256]{1,0:T(8,128)} %get-tuple-element.101, s32[4096]{0:T(1024)S(1)} %broadcast_clamp_fusion.2), kind=kCustom, calls=%fused_computation.clone.1 | custom fusion | bytes 8404992 | tf_op jit(solution)/shard_map/while/body/eval_jaxpr/jit(_take)/gather | solution.py:8
  168.3 4.7 %fusion.5 = f32[512,256]{1,0:T(8,128)S(1)} fusion(f32[4096,256]{1,0:T(8,128)} %gather_fusion, f32[512,8]{1,0:T(8,128)S(1)} %dynamic-slice_bitcast_fusion.2, pred[512,8]{1,0:T(8,128)(4,1)S(1)} %compare_and_fusion.2), kind=kLoop, calls=%fused_computation.3.clone.1 | loop fusion | flops 3014656 | bytes 4739072 | tf_op jit(solution)/shard_map/while/body/eval_jaxpr/reduce_sum | solution.py:9
  174.1 18.3 %gather_fusion = f32[4096,256]{1,0:T(8,128)} fusion(f32[4096,256]{1,0:T(8,128)} %get-tuple-element.101, s32[4096]{0:T(1024)S(1)} %broadcast_clamp_fusion.2), kind=kCustom, calls=%fused_computation.clone.1 | custom fusion | bytes 8404992 | tf_op jit(solution)/shard_map/while/body/eval_jaxpr/jit(_take)/gather | solution.py:8
  193.4 4.7 %fusion.5 = f32[512,256]{1,0:T(8,128)S(1)} fusion(f32[4096,256]{1,0:T(8,128)} %gather_fusion, f32[512,8]{1,0:T(8,128)S(1)} %dynamic-slice_bitcast_fusion.2, pred[512,8]{1,0:T(8,128)(4,1)S(1)} %compare_and_fusion.2), kind=kLoop, calls=%fused_computation.3.clone.1 | loop fusion | flops 3014656 | bytes 4739072 | tf_op jit(solution)/shard_map/while/body/eval_jaxpr/reduce_sum | solution.py:9
  199.2 18.3 %gather_fusion = f32[4096,256]{1,0:T(8,128)} fusion(f32[4096,256]{1,0:T(8,128)} %get-tuple-element.101, s32[4096]{0:T(1024)S(1)} %broadcast_clamp_fusion.2), kind=kCustom, calls=%fused_computation.clone.1 | custom fusion | bytes 8404992 | tf_op jit(solution)/shard_map/while/body/eval_jaxpr/jit(_take)/gather | solution.py:8
  218.5 4.7 %fusion.5 = f32[512,256]{1,0:T(8,128)S(1)} fusion(f32[4096,256]{1,0:T(8,128)} %gather_fusion, f32[512,8]{1,0:T(8,128)S(1)} %dynamic-slice_bitcast_fusion.2, pred[512,8]{1,0:T(8,128)(4,1)S(1)} %compare_and_fusion.2), kind=kLoop, calls=%fused_computation.3.clone.1 | loop fusion | flops 3014656 | bytes 4739072 | tf_op jit(solution)/shard_map/while/body/eval_jaxpr/reduce_sum | solution.py:9
  224.1 7.1 %reshape.48 = f32[4096,1,256]{2,1,0:T(1,128)} reshape(f32[8,512,256]{2,1,0:T(8,128)} %get-tuple-element.32) | data formatting | bytes 8388608 | tf_op jit(solution)/shard_map/reshape | solution.py:44
  231.2 96.4 %all_to_all.36 = f32[4096,1,256]{2,1,0:T(1,128)S(1)} all-to-all(f32[4096,1,256]{2,1,0:T(1,128)} %reshape.48), channel_id=1, replica_groups=mesh['group'=8,'local'=4] {'group','local'}, dimensions={0} | all-to-all | bytes 8388608 | tf_op jit(solution)/shard_map/all_to_all | solution.py:45
  327.9 4.4 %copy.13 = f32[128,32,256]{2,1,0:T(8,128)} copy(f32[128,32,256]{2,0,1:T(8,128)S(1)} %bitcast.40) | data formatting | bytes 8388608 | tf_op jit(solution)/shard_map/all_to_all | solution.py:45
  (55 shorter events, 19.2 us)
Async XLA Ops:
  2.6 17.9 %all-to-all-start = ((f32[128,32,16]{0,2,1:T(8,128)}), f32[128,32,16]{0,2,1:T(8,128)S(1)}, u32[]{:S(2)}, u32[]{:S(2)}) async-start(f32[128,32,16]{0,2,1:T(8,128)} %pad_maximum_fusion), calls=%async_computation | async-start | bytes 524288 | tf_op jit(solution)/shard_map/all_to_all | solution.py:31
where the time goes:
time: 334 us; the launch traced here: 332 us
  local copies, waits for them, and re-layouts  176 us (53%)
  blocking collectives  96.4 us (29%)
  other arithmetic  41.6 us (12%)
  waiting for transfers between devices  10.6 us (3%)
  starting transfers between devices  7.33 us (2%)
    gather x8, local copies, waits for them, and re-layouts, pool_block(): rows = jnp.take(table, pair[0], axis=0)  146 us
    all_to_all x1, blocking collectives, body(): lax.all_to_all(pooled, ('group', 'local'), split_axis=0, concat_axis=1, t...  96.4 us
    reduce_sum x8, other arithmetic, pool_block(): return jnp.sum(rows * pair[1][:, :, None], axis=1)  38 us
    all_to_all x1, waiting for transfers between devices, body(): lax.all_to_all(packed, ('group', 'local'), split_axis=1, concat_axis=0, t...  10.6 us
    mul x8, local copies, waits for them, and re-layouts, pool_block(): return jnp.sum(rows * pair[1][:, :, None], axis=1)  7.79 us
    all_to_all x1, starting transfers between devices, body(): lax.all_to_all(packed, ('group', 'local'), split_axis=1, concat_axis=0, t...  7.33 us
    reshape x1, local copies, waits for them, and re-layouts, body(): pooled = pooled.reshape(devices * examples, tab_dev, width)  7.09 us
  transfers between devices with their start and end apart: 1, of which 1 were waited for; matrix products, arithmetic and copies ran while one was open for 0% of the time, Pallas kernels for 0%

commit v1 on v0

--- a/solution.py
+++ b/solution.py
@@ -42,7 +42,15 @@
         (index.reshape(blocks, block_rows, bag), weights.reshape(blocks, block_rows, bag)),
     )
     pooled = pooled.reshape(devices * examples, tab_dev, width)
-    result = lax.all_to_all(pooled, ("group", "local"), split_axis=0, concat_axis=1, tiled=True)
+    result = jnp.concatenate(
+        lax.all_to_all(
+            jnp.stack(jnp.split(pooled, lax.axis_size(("group", "local")), axis=0)),
+            ("group", "local"),
+            0,
+            0,
+        ),
+        axis=1,
+    )
     return result
 
 

time: 334 us -> 356 us (1.066)
  local copies, waits for them, and re-layouts: 176 us -> 198 us
    unnamed x1 -> x31, local copies, waits for them, and re-layouts: 0.27 us -> 28.4 us
    all_to_all x1 -> x0, local copies, waits for them, and re-layouts: 4.44 us -> none  [body(): lax.all_to_all(pooled, ('group', 'local'), split_axis=0, concat_axis=1, t...]
where the time goes in v1:
time: 356 us; the launch traced here: 354 us
  local copies, waits for them, and re-layouts  198 us (56%)
  blocking collectives  95.8 us (27%)
  other arithmetic  41.6 us (12%)
  waiting for transfers between devices  10.6 us (3%)
  starting transfers between devices  7.33 us (2%)
    gather x8, local copies, waits for them, and re-layouts, pool_block(): rows = jnp.take(table, pair[0], axis=0)  146 us
    all_to_all x1, blocking collectives, body(): lax.all_to_all(jnp.stack(jnp.split(pooled, lax.axis_size(('group', 'local...  95.8 us
    reduce_sum x8, other arithmetic, pool_block(): return jnp.sum(rows * pair[1][:, :, None], axis=1)  38 us
    unnamed x31, local copies, waits for them, and re-layouts  28.4 us
    all_to_all x1, waiting for transfers between devices, body(): lax.all_to_all(packed, ('group', 'local'), split_axis=1, concat_axis=0, t...  10.6 us
    mul x8, local copies, waits for them, and re-layouts, pool_block(): return jnp.sum(rows * pair[1][:, :, None], axis=1)  7.79 us
    all_to_all x1, starting transfers between devices, body(): lax.all_to_all(packed, ('group', 'local'), split_axis=1, concat_axis=0, t...  7.33 us
  transfers between devices with their start and end apart: 1, of which 1 were waited for; matrix products, arithmetic and copies ran while one was open for 0% of the time, Pallas kernels for 0%

profile of v1, /device:TPU:0, one launch (start us, length us, event | category | flops | bytes accessed | tf_op | source)
XLA Modules:
  0.0 353.8 jit_solution(16742254887787897076)
XLA Ops:
  2.6 7.3 %all-to-all-start = ((f32[128,32,16]{0,2,1:T(8,128)}), f32[128,32,16]{0,2,1:T(8,128)S(1)}, u32[]{:S(2)}, u32[]{:S(2)}) async-start(f32[128,32,16]{0,2,1:T(8,128)} %pad_maximum_fusion), calls=%async_computation | async-start | bytes 524288 | tf_op jit(solution)/shard_map/all_to_all | solution.py:31
  9.9 10.6 %all-to-all-done = f32[128,32,16]{0,2,1:T(8,128)S(1)} async-done(((f32[128,32,16]{0,2,1:T(8,128)}), f32[128,32,16]{0,2,1:T(8,128)S(1)}, u32[]{:S(2)}, u32[]{:S(2)}) %all-to-all-start) | async-done | bytes 262176 | tf_op jit(solution)/shard_map/all_to_all | solution.py:31
  20.7 1.9 copy.76
  23.2 200.9 %while.10 = (s32[]{:T(128)}, f32[8,512,256]{2,1,0:T(8,128)}, s32[8,512,8]{2,1,0:T(8,128)S(1)}, f32[4096,256]{1,0:T(8,128)}, f32[8,512,8]{2,1,0:T(8,128)}, /*index=5*/s32[]{:T(128)}) while((s32[]{:T(128)}, f32[8,512,256]{2,1,0:T(8,128)}, s32[8,512,8]{2,1,0:T(8,128)S(1)}, f32[4096,256]{1,0:T(8,128)}, f32[8,512,8]{2,1,0:T(8,128)}, ...), condition=%wide.region_2.3_spmd, body=%wide.region_0.2_spmd.sunk | while | flops 3055618 | bytes 14344785 | solution.py:40
  23.4 18.3 %gather_fusion = f32[4096,256]{1,0:T(8,128)} fusion(f32[4096,256]{1,0:T(8,128)} %get-tuple-element.101, s32[4096]{0:T(1024)S(1)} %broadcast_clamp_fusion.2), kind=kCustom, calls=%fused_computation.clone.1 | custom fusion | bytes 8404992 | tf_op jit(solution)/shard_map/while/body/eval_jaxpr/jit(_take)/gather | solution.py:8
  42.8 4.7 %fusion.37 = f32[512,256]{1,0:T(8,128)S(1)} fusion(f32[4096,256]{1,0:T(8,128)} %gather_fusion, f32[512,8]{1,0:T(8,128)S(1)} %dynamic-slice_bitcast_fusion.2, pred[512,8]{1,0:T(8,128)(4,1)S(1)} %compare_and_fusion.2), kind=kLoop, calls=%fused_computation.3.clone.1 | loop fusion | flops 3014656 | bytes 4739072 | tf_op jit(solution)/shard_map/while/body/eval_jaxpr/reduce_sum | solution.py:9
  48.5 18.3 %gather_fusion = f32[4096,256]{1,0:T(8,128)} fusion(f32[4096,256]{1,0:T(8,128)} %get-tuple-element.101, s32[4096]{0:T(1024)S(1)} %broadcast_clamp_fusion.2), kind=kCustom, calls=%fused_computation.clone.1 | custom fusion | bytes 8404992 | tf_op jit(solution)/shard_map/while/body/eval_jaxpr/jit(_take)/gather | solution.py:8
  67.9 4.7 %fusion.37 = f32[512,256]{1,0:T(8,128)S(1)} fusion(f32[4096,256]{1,0:T(8,128)} %gather_fusion, f32[512,8]{1,0:T(8,128)S(1)} %dynamic-slice_bitcast_fusion.2, pred[512,8]{1,0:T(8,128)(4,1)S(1)} %compare_and_fusion.2), kind=kLoop, calls=%fused_computation.3.clone.1 | loop fusion | flops 3014656 | bytes 4739072 | tf_op jit(solution)/shard_map/while/body/eval_jaxpr/reduce_sum | solution.py:9
  73.6 18.3 %gather_fusion = f32[4096,256]{1,0:T(8,128)} fusion(f32[4096,256]{1,0:T(8,128)} %get-tuple-element.101, s32[4096]{0:T(1024)S(1)} %broadcast_clamp_fusion.2), kind=kCustom, calls=%fused_computation.clone.1 | custom fusion | bytes 8404992 | tf_op jit(solution)/shard_map/while/body/eval_jaxpr/jit(_take)/gather | solution.py:8
  92.0 1.0 dynamic-slice_bitcast_fusion.2
  93.0 4.7 %fusion.37 = f32[512,256]{1,0:T(8,128)S(1)} fusion(f32[4096,256]{1,0:T(8,128)} %gather_fusion, f32[512,8]{1,0:T(8,128)S(1)} %dynamic-slice_bitcast_fusion.2, pred[512,8]{1,0:T(8,128)(4,1)S(1)} %compare_and_fusion.2), kind=kLoop, calls=%fused_computation.3.clone.1 | loop fusion | flops 3014656 | bytes 4739072 | tf_op jit(solution)/shard_map/while/body/eval_jaxpr/reduce_sum | solution.py:9
  98.8 18.3 %gather_fusion = f32[4096,256]{1,0:T(8,128)} fusion(f32[4096,256]{1,0:T(8,128)} %get-tuple-element.101, s32[4096]{0:T(1024)S(1)} %broadcast_clamp_fusion.2), kind=kCustom, calls=%fused_computation.clone.1 | custom fusion | bytes 8404992 | tf_op jit(solution)/shard_map/while/body/eval_jaxpr/jit(_take)/gather | solution.py:8
  117.1 1.0 dynamic-slice_bitcast_fusion.2
  118.1 4.7 %fusion.37 = f32[512,256]{1,0:T(8,128)S(1)} fusion(f32[4096,256]{1,0:T(8,128)} %gather_fusion, f32[512,8]{1,0:T(8,128)S(1)} %dynamic-slice_bitcast_fusion.2, pred[512,8]{1,0:T(8,128)(4,1)S(1)} %compare_and_fusion.2), kind=kLoop, calls=%fused_computation.3.clone.1 | loop fusion | flops 3014656 | bytes 4739072 | tf_op jit(solution)/shard_map/while/body/eval_jaxpr/reduce_sum | solution.py:9
  123.9 18.3 %gather_fusion = f32[4096,256]{1,0:T(8,128)} fusion(f32[4096,256]{1,0:T(8,128)} %get-tuple-element.101, s32[4096]{0:T(1024)S(1)} %broadcast_clamp_fusion.2), kind=kCustom, calls=%fused_computation.clone.1 | custom fusion | bytes 8404992 | tf_op jit(solution)/shard_map/while/body/eval_jaxpr/jit(_take)/gather | solution.py:8
  143.2 4.7 %fusion.37 = f32[512,256]{1,0:T(8,128)S(1)} fusion(f32[4096,256]{1,0:T(8,128)} %gather_fusion, f32[512,8]{1,0:T(8,128)S(1)} %dynamic-slice_bitcast_fusion.2, pred[512,8]{1,0:T(8,128)(4,1)S(1)} %compare_and_fusion.2), kind=kLoop, calls=%fused_computation.3.clone.1 | loop fusion | flops 3014656 | bytes 4739072 | tf_op jit(solution)/shard_map/while/body/eval_jaxpr/reduce_sum | solution.py:9
  149.0 18.3 %gather_fusion = f32[4096,256]{1,0:T(8,128)} fusion(f32[4096,256]{1,0:T(8,128)} %get-tuple-element.101, s32[4096]{0:T(1024)S(1)} %broadcast_clamp_fusion.2), kind=kCustom, calls=%fused_computation.clone.1 | custom fusion | bytes 8404992 | tf_op jit(solution)/shard_map/while/body/eval_jaxpr/jit(_take)/gather | solution.py:8
  168.3 4.7 %fusion.37 = f32[512,256]{1,0:T(8,128)S(1)} fusion(f32[4096,256]{1,0:T(8,128)} %gather_fusion, f32[512,8]{1,0:T(8,128)S(1)} %dynamic-slice_bitcast_fusion.2, pred[512,8]{1,0:T(8,128)(4,1)S(1)} %compare_and_fusion.2), kind=kLoop, calls=%fused_computation.3.clone.1 | loop fusion | flops 3014656 | bytes 4739072 | tf_op jit(solution)/shard_map/while/body/eval_jaxpr/reduce_sum | solution.py:9
  174.1 18.3 %gather_fusion = f32[4096,256]{1,0:T(8,128)} fusion(f32[4096,256]{1,0:T(8,128)} %get-tuple-element.101, s32[4096]{0:T(1024)S(1)} %broadcast_clamp_fusion.2), kind=kCustom, calls=%fused_computation.clone.1 | custom fusion | bytes 8404992 | tf_op jit(solution)/shard_map/while/body/eval_jaxpr/jit(_take)/gather | solution.py:8
  193.4 4.7 %fusion.37 = f32[512,256]{1,0:T(8,128)S(1)} fusion(f32[4096,256]{1,0:T(8,128)} %gather_fusion, f32[512,8]{1,0:T(8,128)S(1)} %dynamic-slice_bitcast_fusion.2, pred[512,8]{1,0:T(8,128)(4,1)S(1)} %compare_and_fusion.2), kind=kLoop, calls=%fused_computation.3.clone.1 | loop fusion | flops 3014656 | bytes 4739072 | tf_op jit(solution)/shard_map/while/body/eval_jaxpr/reduce_sum | solution.py:9
  199.2 18.3 %gather_fusion = f32[4096,256]{1,0:T(8,128)} fusion(f32[4096,256]{1,0:T(8,128)} %get-tuple-element.101, s32[4096]{0:T(1024)S(1)} %broadcast_clamp_fusion.2), kind=kCustom, calls=%fused_computation.clone.1 | custom fusion | bytes 8404992 | tf_op jit(solution)/shard_map/while/body/eval_jaxpr/jit(_take)/gather | solution.py:8
  218.5 4.7 %fusion.37 = f32[512,256]{1,0:T(8,128)S(1)} fusion(f32[4096,256]{1,0:T(8,128)} %gather_fusion, f32[512,8]{1,0:T(8,128)S(1)} %dynamic-slice_bitcast_fusion.2, pred[512,8]{1,0:T(8,128)(4,1)S(1)} %compare_and_fusion.2), kind=kLoop, calls=%fused_computation.3.clone.1 | loop fusion | flops 3014656 | bytes 4739072 | tf_op jit(solution)/shard_map/while/body/eval_jaxpr/reduce_sum | solution.py:9
  253.5 95.8 %all_to_all.23 = f32[32,128,1,256]{3,1,2,0:T(8,128)S(1)} all-to-all(f32[32,128,1,256]{3,1,2,0:T(8,128)S(1)} %fusion.2), channel_id=1, replica_groups=mesh['group'=8,'local'=4] {'group','local'}, dimensions={0} | all-to-all | bytes 8388608 | tf_op jit(solution)/shard_map/all_to_all | solution.py:46
  349.4 4.4 %copy.74 = f32[128,32,256]{2,1,0:T(8,128)} copy(f32[128,32,256]{2,0,1:T(8,128)S(1)} %bitcast.167) | data formatting | bytes 8388608 | tf_op jit(solution)/shard_map/reshape | solution.py:45
  (85 shorter events, 47.3 us)
Async XLA Ops:
  2.6 17.9 %all-to-all-start = ((f32[128,32,16]{0,2,1:T(8,128)}), f32[128,32,16]{0,2,1:T(8,128)S(1)}, u32[]{:S(2)}, u32[]{:S(2)}) async-start(f32[128,32,16]{0,2,1:T(8,128)} %pad_maximum_fusion), calls=%async_computation | async-start | bytes 524288 | tf_op jit(solution)/shard_map/all_to_all | solution.py:31
